TPU v7x, 512 devices: a whole 4x8x8 slice. The times are simulated.
512 devices in a mesh: wide: 64 (over z, y), narrow: 8 (over x, core).
Axes of the slice: x: 4, y: 8, z: 8, core: 2. Of those that a mesh axis runs over, the one named last changes fastest.
Arguments:
- square_grads: bfloat16 [4, 8192, 8192], P(None, 'wide', 'narrow'), may hold values from -8.1 to 8.1
- narrow_grads: bfloat16 [4, 8192, 1024], P(None, 'wide', 'narrow'), may hold values from -8.1 to 8.1
- square_rowstate: float32 [4, 8192], P(None, 'wide'), may hold values from 0.0006 to 0.064
- square_colstate: float32 [4, 8192], P(None, 'narrow'), may hold values from 1e-05 to 2.1
- narrow_rowstate: float32 [4, 8192], P(None, 'wide'), may hold values from 0.0006 to 0.064
- narrow_colstate: float32 [4, 1024], P(None, 'narrow'), may hold values from 1e-05 to 2.1
Outputs:
- square_update: float32 [4, 8192, 8192], P(None, 'wide', 'narrow')
- narrow_update: float32 [4, 8192, 1024], P(None, 'wide', 'narrow')
- square_rowfactor: float32 [4, 8192], P(None, 'wide')
- square_colfactor: float32 [4, 8192], P(None, 'narrow')
- narrow_rowfactor: float32 [4, 8192], P(None, 'wide')
- narrow_colfactor: float32 [4, 1024], P(None, 'narrow')
All inputs are finite; a program needn't handle non-finite values.
Results may differ from a plain program's by a relative error of at most 0.0004.
Values sent between devices are 32-bit elements; how exact they have to be, the bound alone decides.
A program may use at most 64 MiB of HBM per device.

v0:
```python
import jax
import jax.numpy as jnp
from jax import lax
from jax.sharding import Mesh
from jax.sharding import PartitionSpec as P

WIDE = ("wide_0", "wide_1")
NARROW = ("narrow_0", "narrow_1")
WIDE_NARROW = ("wide_0", "wide_1", "narrow_0", "narrow_1")


decay_rate = 0.9
epsilon_square = 1e-30
clip_limit = 1.0


def from_everyone(shard, axis):
    copies = jnp.broadcast_to(shard, (lax.axis_size(axis), *shard.shape))
    return lax.all_to_all(copies, axis, split_axis=0, concat_axis=0, tiled=True)


def of_everyone(shard, axis):
    return from_everyone(shard, axis).sum(axis=0)


def packed_total(arrays, axis):
    ends = [0]
    for a in arrays:
        ends.append(ends[-1] + a.size)
    subtotal = of_everyone(jnp.concatenate([a.ravel() for a in arrays]), axis)
    return tuple((subtotal[b:e].reshape(a.shape) for a, b, e in zip(arrays, ends, ends[1:])))


def by_axis(shard, axes):
    for axis in axes:
        shard = lax.psum(shard, axis)
    return shard


def square_sums(grads):
    values = grads.astype(jnp.float32)
    squares = values * values + epsilon_square
    return (values, jnp.sum(squares, axis=2), jnp.sum(squares, axis=1))


def blend(state, total, count):
    return decay_rate * state + (1.0 - decay_rate) * (total / count)


def scaled(values, rowfactor, colfactor, row_mean):
    return (
        values
        * lax.rsqrt(rowfactor)[:, :, None]
        * lax.rsqrt(colfactor)[:, None, :]
        * jnp.sqrt(row_mean)[:, None, None]
    )


def clipped(raw, norm, entries):
    spread = jnp.sqrt(norm / entries)
    return raw / jnp.maximum(1.0, spread / clip_limit)[:, None, None]


def per_device(
    square_grads, narrow_grads, square_rowstate, square_colstate, narrow_rowstate, narrow_colstate
):
    total_rows = square_grads.shape[1] * lax.axis_size(WIDE)
    square_width = square_grads.shape[2] * lax.axis_size(NARROW)
    narrow_width = narrow_grads.shape[2] * lax.axis_size(NARROW)
    square_values, square_rowpart, square_colpart = square_sums(square_grads)
    narrow_values, narrow_rowpart, narrow_colpart = square_sums(narrow_grads)
    square_colsum, narrow_colsum, square_oldsum, narrow_oldsum = packed_total(
        (
            square_colpart,
            narrow_colpart,
            jnp.sum(square_rowstate, axis=1),
            jnp.sum(narrow_rowstate, axis=1),
        ),
        WIDE,
    )
    square_colfactor = blend(square_colstate, square_colsum, total_rows)
    narrow_colfactor = blend(narrow_colstate, narrow_colsum, total_rows)
    square_rowsum, narrow_rowsum, square_total, narrow_total = packed_total(
        (
            square_rowpart,
            narrow_rowpart,
            jnp.sum(square_colsum, axis=1),
            jnp.sum(narrow_colsum, axis=1),
        ),
        NARROW,
    )
    square_rowfactor = blend(square_rowstate, square_rowsum, square_width)
    narrow_rowfactor = blend(narrow_rowstate, narrow_rowsum, narrow_width)
    square_mean = (
        decay_rate * square_oldsum + (1.0 - decay_rate) * (square_total / square_width)
    ) / total_rows
    narrow_mean = (
        decay_rate * narrow_oldsum + (1.0 - decay_rate) * (narrow_total / narrow_width)
    ) / total_rows
    square_raw = scaled(square_values, square_rowfactor, square_colfactor, square_mean)
    narrow_raw = scaled(narrow_values, narrow_rowfactor, narrow_colfactor, narrow_mean)
    square_norm, narrow_norm = (
        by_axis(jnp.sum(square_raw * square_raw, axis=(1, 2)), WIDE_NARROW),
        by_axis(jnp.sum(narrow_raw * narrow_raw, axis=(1, 2)), WIDE_NARROW),
    )
    square_update = clipped(square_raw, square_norm, total_rows * square_width)
    narrow_update = clipped(narrow_raw, narrow_norm, total_rows * narrow_width)
    return (
        square_update,
        narrow_update,
        square_rowfactor,
        square_colfactor,
        narrow_rowfactor,
        narrow_colfactor,
    )


def solution(mesh):
    torus = Mesh(mesh.devices.reshape(8, 8, 4, 2), ("wide_0", "wide_1", "narrow_0", "narrow_1"))
    in_specs = (
        P(None, WIDE, NARROW),
        P(None, WIDE, NARROW),
        P(None, WIDE),
        P(None, NARROW),
        P(None, WIDE),
        P(None, NARROW),
    )
    out_specs = (
        P(None, WIDE, NARROW),
        P(None, WIDE, NARROW),
        P(None, WIDE),
        P(None, NARROW),
        P(None, WIDE),
        P(None, NARROW),
    )
    return jax.shard_map(
        per_device, mesh=torus, in_specs=in_specs, out_specs=out_specs, check_vma=False
    )
```

profile of v0, /device:TPU:1, one launch (start us, length us, event | category | flops | bytes accessed | tf_op | source)
XLA Modules:
  0.0 115.5 jit_solution(5168812018291472574)
XLA Ops:
  0.6 0.8 reduce_sum.112
  1.4 0.8 reduce_sum.113
  2.2 1.1 fusion.9
  3.3 1.7 %fusion.1 = (f32[4,1024]{1,0:T(4,128)S(1)}, f32[4,128]{1,0:T(4,128)S(1)}) fusion(bf16[4,128,1024]{2,1,0:T(8,128)(2,1)} %param.6), kind=kLoop, calls=%fused_computation.3 | loop fusion | flops 2616832 | bytes 1067008 | tf_op jit(solution)/shard_map/reduce_sum | solution.py:43
  5.0 0.1 concatenate.6
  5.0 0.6 broadcast_in_dim.4
  5.7 0.0 copy-start.5
  5.7 0.0 copy-start.2
  5.7 0.0 copy-start.3
  5.7 0.0 copy-start.4
  5.7 0.0 copy-start
  5.7 0.0 copy-start.1
  5.7 48.1 %all_to_all.12 = f32[64,1,4616]{2,1,0:T(1,128)S(1)} all-to-all(f32[64,1,4616]{2,1,0:T(1,128)S(1)} %broadcast_in_dim.4), channel_id=1, replica_groups=mesh['wide_0'=8,'wide_1'=8,'narrow_0'=4,'narrow_1'=2] {'wide_0','wide_1'}, dimensions={0} | all-to-all | bytes 2363392 | tf_op jit(solution)/shard_map/all_to_all | solution.py:19
  53.9 0.7 reduce_sum.114
  54.6 0.0 copy-done.5
  54.6 0.7 fusion.25
  55.3 0.0 copy-done.2
  55.3 0.7 fusion.28
  56.1 0.1 concatenate.7
  56.2 12.1 %all_to_all.13 = f32[8,1,1032]{2,1,0:T(1,128)S(1)} all-to-all(f32[8,1,1032]{2,1,0:T(1,128)S(1)} %broadcast_in_dim.5), channel_id=1, replica_groups=mesh['wide_0'=8,'wide_1'=8,'narrow_0'=4,'narrow_1'=2] {'narrow_0','narro..., dimensions={0} | all-to-all | bytes 66048 | tf_op jit(solution)/shard_map/all_to_all | solution.py:19
  68.3 0.1 multiply_sqrt_fusion
  68.4 0.0 copy-done.3
  68.4 0.0 copy-done.4
  68.4 0.6 fusion.23
  69.0 0.0 copy-done
  69.0 0.7 fusion.7
  69.6 0.0 copy-done.1
  69.6 0.2 fusion.15
  69.8 12.1 %all-reduce.1 = (f32[4]{0:T(128)S(1)}, f32[4]{0:T(128)S(1)}) all-reduce(f32[4]{0:T(128)S(1)} %fusion.7, f32[4]{0:T(128)S(1)} %fusion.15), channel_id=1, replica_groups=mesh['wide_0'=8,'wide_1'=8,'narrow_0'=4,'narrow_1'=2] {'wide_0'}, use_global_device_ids=true, to_apply=%region_11.0 | all-reduce | flops 8 | bytes 64 | tf_op jit(solution)/shard_map/psum | solution.py:36
  81.9 12.0 %all-reduce = (f32[4]{0:T(128)S(1)}, f32[4]{0:T(128)S(1)}) all-reduce(f32[4]{0:T(128)S(1)} %get-tuple-element.12, f32[4]{0:T(128)S(1)} %get-tuple-element.13), channel_id=1, replica_groups=mesh['wide_0'=8,'wide_1'=8,'narrow_0'=4,'narrow_1'=2] {'wide_1'}, use_global_device_ids=true, to_apply=%region_12.0 | all-reduce | flops 8 | bytes 64 | tf_op jit(solution)/shard_map/psum | solution.py:36
  93.9 6.9 %all-reduce.2 = (f32[4]{0:T(128)S(1)}, f32[4]{0:T(128)S(1)}) all-reduce(f32[4]{0:T(128)S(1)} %get-tuple-element.10, f32[4]{0:T(128)S(1)} %get-tuple-element.11), channel_id=1, replica_groups=mesh['wide_0'=8,'wide_1'=8,'narrow_0'=4,'narrow_1'=2] {'narrow_0'}, use_global_device_ids=true, to_apply=%region_13.0 | all-reduce | flops 8 | bytes 64 | tf_op jit(solution)/shard_map/psum | solution.py:36
  100.8 12.1 %all-reduce.3 = (f32[4]{0:T(128)S(1)}, f32[4]{0:T(128)S(1)}) all-reduce(f32[4]{0:T(128)S(1)} %get-tuple-element.14, f32[4]{0:T(128)S(1)} %get-tuple-element.15), channel_id=1, replica_groups=mesh['wide_0'=8,'wide_1'=8,'narrow_0'=4,'narrow_1'=2] {'narrow_1'}, use_global_device_ids=true, to_apply=%region_14.0 | all-reduce | flops 8 | bytes 64 | tf_op jit(solution)/shard_map/psum | solution.py:36
  112.9 0.9 fusion.13
  113.8 1.7 %fusion.5 = f32[4,128,1024]{2,1,0:T(8,128)} fusion(bf16[4,128,1024]{2,1,0:T(8,128)(2,1)S(1)} %copy-done, f32[4]{0:T(128)S(1)} %get-tuple-element.33, f32[4]{0:T(128)S(1)} %get-tuple-element.27, f32[4,1024]{1,0:T(4,128)S(1)} %get-tuple-element.24, f32[4,128]{1,0:T(4,128)S(1)} %get-tuple-element.30), kind=kLoop, calls=%fused_computation.7 | loop fusion | flops 2621440 | bytes 3164192 | tf_op jit(solution)/shard_map/div | solution.py:61
  (6 shorter events, 0.1 us)
Async XLA Ops:
  5.7 49.0 %copy-start.5 = (f32[4,128]{1,0:T(4,128)S(1)}, f32[4,128]{1,0:T(4,128)}, u32[]{:S(2)}) copy-start(f32[4,128]{1,0:T(4,128)} %param.11) | copy-start | bytes 6148
  5.7 49.7 %copy-start.2 = (f32[4,1024]{1,0:T(4,128)S(1)}, f32[4,1024]{1,0:T(4,128)}, u32[]{:S(2)}) copy-start(f32[4,1024]{1,0:T(4,128)} %param.9) | copy-start | bytes 49156
  5.7 62.7 %copy-start.3 = (f32[4,128]{1,0:T(4,128)S(1)}, f32[4,128]{1,0:T(4,128)}, u32[]{:S(2)}) copy-start(f32[4,128]{1,0:T(4,128)} %param.8) | copy-start | bytes 6148
  5.7 62.7 %copy-start.4 = (f32[4,128]{1,0:T(4,128)S(1)}, f32[4,128]{1,0:T(4,128)}, u32[]{:S(2)}) copy-start(f32[4,128]{1,0:T(4,128)} %param.10) | copy-start | bytes 6148
  5.7 63.2 %copy-start = (bf16[4,128,1024]{2,1,0:T(8,128)(2,1)S(1)}, bf16[4,128,1024]{2,1,0:T(8,128)(2,1)}, u32[]{:S(2)}) copy-start(bf16[4,128,1024]{2,1,0:T(8,128)(2,1)} %param.6) | copy-start | bytes 3145732
  5.7 63.9 %copy-start.1 = (bf16[4,128,128]{2,1,0:T(8,128)(2,1)S(1)}, bf16[4,128,128]{2,1,0:T(8,128)(2,1)}, u32[]{:S(2)}) copy-start(bf16[4,128,128]{2,1,0:T(8,128)(2,1)} %param.7) | copy-start | bytes 393220
where the time goes:
time: 116 us
  blocking collectives  103 us (89%)
  other arithmetic  10.7 us (9%)
    all_to_all x2, blocking collectives, from_everyone(): return lax.all_to_all(copies, axis, split_axis=0, concat_axis=0, tiled=True)  60.2 us
    psum x4, blocking collectives, by_axis(): shard = lax.psum(shard, axis)  43.1 us
    reduce_sum x2, other arithmetic, square_sums(): return (values, jnp.sum(squares, axis=2), jnp.sum(squares, axis=1))  2.71 us
    div x2, other arithmetic, clipped(): return raw / jnp.maximum(1.0, spread / clip_limit)[:, None, None]  2.59 us

commit v1 on v0

v1 whole, which is shorter than its diff:
```python
import functools

import jax
import jax.numpy as jnp
from jax import lax
from jax.experimental import pallas as pl
from jax.experimental.pallas import tpu as pltpu
from jax.sharding import Mesh
from jax.sharding import PartitionSpec as P

WIDE = ("wide_0", "wide_1")
NARROW = ("narrow_0", "narrow_1")
MESH = pl.DeviceIdType.MESH

decay_rate = 0.9
epsilon_square = 1e-30
clip_limit = 1.0

f32 = jnp.float32

ROWS, CZ, CY, WZ, WY, AG, SZ, SN = range(8)
FAR_FIRST = (4, 3, 5, 2, 6, 1, 7)


def exchange_kernel(
    gs, gn, rs, rn, cs, cn,
    ts, tn, rowf, colfs, colfn, cscs, cscn,
    vs, vn, vrs, vrn, vcs, vcn, part, rb,
    rows_buf, c_out, w_out, cz, cy, wz, wy, ag, sz, sn,
    load_sem, send_sem, recv_sem,
):
    z, y = lax.axis_index("wide_0"), lax.axis_index("wide_1")
    x, core = lax.axis_index("narrow_0"), lax.axis_index("narrow_1")

    def on_z(d):
        return {"wide_0": lax.rem(z + d, 8)}

    def on_y(d):
        return {"wide_1": lax.rem(y + d, 8)}

    def on_narrow(d):
        return {"narrow_0": lax.rem(x + d // 2, 4), "narrow_1": lax.rem(core + d % 2, 2)}

    loads = [pltpu.make_async_copy(gs.at[m], vs.at[m], load_sem.at[m]) for m in range(4)]
    loads.append(pltpu.make_async_copy(gn, vn, load_sem.at[4]))
    for i, (a, b) in enumerate(((rs, vrs), (rn, vrn), (cs, vcs), (cn, vcn))):
        loads.append(pltpu.make_async_copy(a, b, load_sem.at[5 + i]))
    for c in loads:
        c.start()

    barrier = pltpu.get_barrier_semaphore()
    for d in FAR_FIRST:
        for peer in (on_z(d), on_y(d), on_narrow(d)):
            pl.semaphore_signal(barrier, inc=1, device_id=peer, device_id_type=MESH)

    def send(kind, d, src, dst, peer):
        c = pltpu.make_async_remote_copy(
            src_ref=src, dst_ref=dst, send_sem=send_sem.at[kind, d], recv_sem=recv_sem.at[kind, d],
            device_id=peer, device_id_type=MESH)
        c.start()
        return c

    started = []

    def column_sums(m, ref, width):
        blocks = width // 128

        def step(r, acc):
            rows = pl.ds(r * 16, 16)
            v = ref[rows, :].astype(f32)
            q = v * v
            p = q[:, 0:128]
            for b in range(1, blocks):
                p = p + q[:, b * 128:(b + 1) * 128]
            part[m, rows, :] = p
            return acc + (q[0:8] + q[8:16])

        acc = lax.fori_loop(0, 8, step, jnp.zeros((8, width), f32), unroll=True)
        return jnp.sum(acc, axis=0, keepdims=True)

    for m in range(4):
        loads[m].wait()
        total = column_sums(m, vs.at[m], 1024)
        for k in range(8):
            c_out[k, m:m + 1, :] = total[:, k * 128:(k + 1) * 128]
    loads[4].wait()
    for m in range(4):
        total = column_sums(4 + m, vn.at[m], 128)
        c_out[m, 4:5, :] = total
        c_out[m + 4, 4:5, :] = total
    for m in range(8):
        rows_buf[0, m:m + 1, :] = jnp.sum(part[m].T, axis=0, keepdims=True)

    pl.semaphore_wait(barrier, 21)

    row_copies = [send(ROWS, d, rows_buf.at[0], rows_buf.at[d], on_narrow(d)) for d in FAR_FIRST]
    cz[0] = c_out[z]
    cz_copies = [send(CZ, d, c_out.at[lax.rem(z + d, 8)], cz.at[d], on_z(d)) for d in FAR_FIRST]
    started += row_copies + cz_copies

    for c in loads[5:]:
        c.wait()

    for c in row_copies:
        c.wait_recv()
    rowsum = None
    for sx in range(4):
        for sc in range(2):
            slot = lax.rem(x + 4 - sx, 4) * 2 + lax.rem(core + sc, 2)
            piece = rows_buf[slot]
            rowsum = piece if rowsum is None else rowsum + piece
    sub = lax.broadcasted_iota(jnp.int32, (8, 128), 0)
    lane = lax.broadcasted_iota(jnp.int32, (8, 128), 1)
    rowf[0:4, :] = decay_rate * vrs[...] + (1.0 - decay_rate) * (rowsum[0:4] / 8192 + epsilon_square)
    rowf[4:8, :] = decay_rate * vrn[...] + (1.0 - decay_rate) * (rowsum[4:8] / 1024 + epsilon_square)
    factor = rowf[...]
    inverse = lax.rsqrt(factor)
    for m in range(8):
        rb[m] = jnp.broadcast_to(inverse[m:m + 1, :], (128, 128)).T
    totals = jnp.sum(factor, axis=1, keepdims=True)
    totals = jnp.sum(jnp.where(lane == sub, totals, 0.0), axis=0, keepdims=True)
    for k in range(8):
        w_out[k, 5:6, :] = totals

    def weighted_sums(m, ref, out, width):
        blocks = width // 128

        def step(r, acc):
            rows = pl.ds(r * 16, 16)
            scale = rb[m, rows, :]
            v = ref[rows, :].astype(f32)
            new = []
            for b in range(blocks):
                t = v[:, b * 128:(b + 1) * 128] * scale
                out[rows, b * 128:(b + 1) * 128] = t
                q = t * t
                new.append(acc[b] + (q[0:8] + q[8:16]))
            return tuple(new)

        acc = lax.fori_loop(0, 8, step, tuple(jnp.zeros((8, 128), f32) for _ in range(blocks)), unroll=True)
        return [jnp.sum(a, axis=0, keepdims=True) for a in acc]

    for m in range(4):
        total = weighted_sums(m, vs.at[m], ts.at[m], 1024)
        for k in range(8):
            w_out[k, m:m + 1, :] = total[k]
    for m in range(4):
        total = weighted_sums(4 + m, vn.at[m], tn.at[m], 128)[0]
        w_out[m, 4:5, :] = total
        w_out[m + 4, 4:5, :] = total

    wz[0] = w_out[z]
    wz_copies = [send(WZ, d, w_out.at[lax.rem(z + d, 8)], wz.at[d], on_z(d)) for d in FAR_FIRST]
    started += wz_copies

    def gathered(buf, me, copies):
        for c in copies:
            c.wait_recv()
        total = None
        for s in range(8):
            piece = buf[lax.rem(me + 8 - s, 8)]
            total = piece if total is None else total + piece
        return total

    cy[0] = gathered(cz, z, cz_copies)
    cy_copies = [send(CY, d, cy.at[0], cy.at[d], on_y(d)) for d in FAR_FIRST]
    started += cy_copies

    wy[0] = gathered(wz, z, wz_copies)
    wy_copies = [send(WY, d, wy.at[0], wy.at[d], on_y(d)) for d in FAR_FIRST]
    started += wy_copies

    colsum = gathered(cy, y, cy_copies)
    state = vcs[:, pl.ds(pl.multiple_of(z * 128, 128), 128)]
    ag[0, 0:4, :] = decay_rate * state + (1.0 - decay_rate) * (colsum[0:4] / 8192 + epsilon_square)
    ag[0, 4:5, :] = (decay_rate * vcn[pl.ds(lax.rem(z, 4), 1), :]
                     + (1.0 - decay_rate) * (colsum[4:5] / 8192 + epsilon_square))
    ag_copies = [send(AG, d, ag.at[0], ag.at[d], on_z(d)) for d in FAR_FIRST]
    started += ag_copies
    own = ag[0]

    weighted = gathered(wy, y, wy_copies)
    share = jnp.sum(weighted[0:5] / own, axis=1, keepdims=True)
    sub5, lane5 = sub[0:5], lane[0:5]
    target = jnp.where(sub5 == 4, 4 + z, sub5)
    share = jnp.sum(jnp.where(lane5 == target, share, 0.0), axis=0, keepdims=True)
    sz[0] = share
    sz_copies = [send(SZ, d, sz.at[0], sz.at[d], on_z(d)) for d in FAR_FIRST]
    started += sz_copies

    for c in ag_copies:
        c.wait_recv()
    for s in range(8):
        piece = ag[lax.rem(z + 8 - s, 8)]
        colfs[:, s * 128:(s + 1) * 128] = piece[0:4]
        if s < 4:
            colfn[s:s + 1, :] = piece[4:5]
    inv_s, inv_n = lax.rsqrt(colfs[...]), lax.rsqrt(colfn[...])

    sn[0] = gathered(sz, z, sz_copies)
    sn_copies = [send(SN, d, sn.at[0], sn.at[d], on_narrow(d)) for d in FAR_FIRST]
    started += sn_copies
    for c in sn_copies:
        c.wait_recv()
    norm = sn[0]
    for d in range(1, 8):
        norm = norm + sn[d]
    lane1 = lane[0:1]
    entries = jnp.where(lane1 < 4, 8192.0 * 8192.0, 8192.0 * 1024.0)
    row_mean = weighted[5:6] / 8192
    spread = jnp.sqrt(row_mean * norm / entries)
    scale = jnp.sqrt(row_mean) / jnp.maximum(1.0, spread / clip_limit)
    scale = jnp.sum(jnp.where(lane == sub, jnp.broadcast_to(scale, (8, 128)), 0.0), axis=1, keepdims=True)
    cscs[...] = inv_s * scale[0:4]
    cscn[...] = inv_n * scale[4:8]

    for c in started:
        c.wait_send()


def output_kernel(
    ts, tn, rowf, colfs, colfn, cscs, cscn,
    us, un, rfs, cfs, rfn, cfn,
    bs, bn, brs, brn, sem,
):
    brs[...] = rowf[0:4, :]
    brn[...] = rowf[4:8, :]
    copies = [
        pltpu.make_async_copy(brs, rfs, sem.at[5]),
        pltpu.make_async_copy(brn, rfn, sem.at[6]),
        pltpu.make_async_copy(colfs, cfs, sem.at[7]),
        pltpu.make_async_copy(colfn, cfn, sem.at[8]),
    ]
    for c in copies:
        c.start()
    for m in range(4):
        bs[m] = ts[m] * cscs[m:m + 1, :]
        c = pltpu.make_async_copy(bs.at[m], us.at[m], sem.at[m])
        c.start()
        copies.append(c)
    for m in range(4):
        bn[m] = tn[m] * cscn[m:m + 1, :]
    c = pltpu.make_async_copy(bn, un, sem.at[4])
    c.start()
    copies.append(c)
    for c in copies:
        c.wait()


def per_device(
    square_grads, narrow_grads, square_rowstate, square_colstate, narrow_rowstate, narrow_colstate
):
    hbm = pl.BlockSpec(memory_space=pltpu.HBM)
    vmem = pl.BlockSpec(memory_space=pltpu.VMEM)
    V = pltpu.VMEM
    middle = pl.pallas_call(
        exchange_kernel,
        out_shape=[
            jax.ShapeDtypeStruct((4, 128, 1024), f32), jax.ShapeDtypeStruct((4, 128, 128), f32),
            jax.ShapeDtypeStruct((8, 128), f32),
            jax.ShapeDtypeStruct((4, 1024), f32), jax.ShapeDtypeStruct((4, 128), f32),
            jax.ShapeDtypeStruct((4, 1024), f32), jax.ShapeDtypeStruct((4, 128), f32),
        ],
        in_specs=[hbm] * 6,
        out_specs=[vmem] * 7,
        scratch_shapes=[
            V((4, 128, 1024), jnp.bfloat16), V((4, 128, 128), jnp.bfloat16),
            V((4, 128), f32), V((4, 128), f32), V((4, 1024), f32), V((4, 128), f32),
            V((8, 128, 128), f32), V((8, 128, 128), f32),
            V((8, 8, 128), f32),
            V((8, 5, 128), f32), V((8, 6, 128), f32),
            V((8, 5, 128), f32), V((8, 5, 128), f32),
            V((8, 6, 128), f32), V((8, 6, 128), f32),
            V((8, 5, 128), f32), V((8, 1, 128), f32), V((8, 1, 128), f32),
            pltpu.SemaphoreType.DMA((9,)),
            pltpu.SemaphoreType.DMA((8, 8)),
            pltpu.SemaphoreType.DMA((8, 8)),
        ],
        compiler_params=pltpu.CompilerParams(
            collective_id=0, has_side_effects=True, vmem_limit_bytes=24 * 2**20),
        name="exchange",
    )(*(pltpu.with_memory_space_constraint(a, pltpu.HBM) for a in (
        square_grads, narrow_grads, square_rowstate, narrow_rowstate, square_colstate, narrow_colstate)))
    us, un, rfs, cfs, rfn, cfn = pl.pallas_call(
        output_kernel,
        out_shape=[
            jax.ShapeDtypeStruct((4, 128, 1024), f32), jax.ShapeDtypeStruct((4, 128, 128), f32),
            jax.ShapeDtypeStruct((4, 128), f32), jax.ShapeDtypeStruct((4, 1024), f32),
            jax.ShapeDtypeStruct((4, 128), f32), jax.ShapeDtypeStruct((4, 128), f32),
        ],
        in_specs=[vmem] * 7,
        out_specs=[hbm] * 6,
        scratch_shapes=[
            V((4, 128, 1024), f32), V((4, 128, 128), f32), V((4, 128), f32), V((4, 128), f32),
            pltpu.SemaphoreType.DMA((9,)),
        ],
        compiler_params=pltpu.CompilerParams(vmem_limit_bytes=24 * 2**20),
        name="output",
    )(*middle)
    return us, un, rfs, cfs, rfn, cfn


def solution(mesh):
    torus = Mesh(mesh.devices.reshape(8, 8, 4, 2), ("wide_0", "wide_1", "narrow_0", "narrow_1"))
    in_specs = (
        P(None, WIDE, NARROW),
        P(None, WIDE, NARROW),
        P(None, WIDE),
        P(None, NARROW),
        P(None, WIDE),
        P(None, NARROW),
    )
    out_specs = (
        P(None, WIDE, NARROW),
        P(None, WIDE, NARROW),
        P(None, WIDE),
        P(None, NARROW),
        P(None, WIDE),
        P(None, NARROW),
    )
    return jax.shard_map(
        per_device, mesh=torus, in_specs=in_specs, out_specs=out_specs, check_vma=False
    )
```

time: 116 us -> 39 us (0.34)
  blocking collectives: 103 us -> 0 us
  Pallas kernels: 0 us -> 38.2 us
  other arithmetic: 10.7 us -> 0 us
    all_to_all x2 -> x0, blocking collectives: 60.2 us -> none  [from_everyone(): return lax.all_to_all(copies, axis, split_axis=0, concat_axis=0, tiled=True)]
    psum x4 -> x0, blocking collectives: 43.1 us -> none  [by_axis(): shard = lax.psum(shard, axis)]
    pallas_call x0 -> x2, Pallas kernels: none -> 38.2 us  [the longest x1 36.7 us: per_device(): pl.pallas_call(exchange_kernel, out_shape=[jax.ShapeDtypeStruct((4, 128,...]
    reduce_sum x8 -> x0, other arithmetic: 5.96 us -> none  [the longest x2 2.71 us: square_sums(): return (values, jnp.sum(squares, axis=2), jnp.sum(squares, axis=1))]
    div x2 -> x0, other arithmetic: 2.59 us -> none  [clipped(): return raw / jnp.maximum(1.0, spread / clip_limit)[:, None, None]]
    rsqrt x3 -> x0, other arithmetic: 2.01 us -> none  [the longest x2 1.42 us: scaled(): lax.rsqrt(colfactor)[:, None, :]]
where the time goes in v1:
time: 39 us; the launch traced here: 38.8 us
  Pallas kernels  38.2 us (98%)
  between operations  0.64 us (2%)
    pallas_call x1, Pallas kernels, per_device(): pl.pallas_call(exchange_kernel, out_shape=[jax.ShapeDtypeStruct((4, 128,...  36.7 us
    pallas_call x1, Pallas kernels, per_device(): pl.pallas_call(output_kernel, out_shape=[jax.ShapeDtypeStruct((4, 128, 10...  1.51 us

profile of v1, /device:TPU:1, one launch (start us, length us, event | category | flops | bytes accessed | tf_op | source)
XLA Modules:
  0.0 38.8 jit_solution(17639462081657543500)
XLA Ops:
  0.6 36.7 %exchange.1 = (f32[4,128,1024]{2,1,0:T(8,128)S(1)}, f32[4,128,128]{2,1,0:T(8,128)S(1)}, f32[8,128]{1,0:T(8,128)S(1)}, f32[4,1024]{1,0:T(4,128)S(1)}, f32[4,128]{...) custom-call(bf16[4,128,1024]{2,1,0:T(8,128)(2,1)} %gs.1, bf16[4,128,128]{2,1,0:T(8,128)(2,1)} %gn.1, ...), custom_call_target="tpu_custom_call" | custom-call | tf_op jit(solution)/shard_map/exchange/pallas_call | solution.py:256
  37.3 1.5 %output.1 = (f32[4,128,1024]{2,1,0:T(8,128)}, f32[4,128,128]{2,1,0:T(8,128)}, f32[4,128]{1,0:T(4,128)}, f32[4,1024]{1,0:T(4,128)}, f32[4,128]{1,0:T(4,128)}, /*index=5*/f32[4,128]{1,0:T(4,128)}) custom-call(f32[4,128,1024]{2,1,0:T(8,128)S(1)} %get-tuple-element.13.ts, f32[4,128,128]{2,1,0:T(8,128)S(1)} %get-tuple-element.14.tn, ...), custom_call_target="tpu_custom_call" | custom-call | tf_op jit(solution)/shard_map/output/pallas_call | solution.py:284

commit v2 on v1

--- a/solution.py
+++ b/solution.py
@@ -18,19 +18,28 @@
 
 f32 = jnp.float32
 
-ROWS, CZ, CY, WZ, WY, AG, SZ, SN = range(8)
+ROWS, CZ, CY, WZ, WY, AG, SX = range(7)
 FAR_FIRST = (4, 3, 5, 2, 6, 1, 7)
+
+OWNERS = 4
+OFFSET = 0
+BLOCKS = 8 // OWNERS
+NARROWS = max(1, 4 // OWNERS)
+CR = 4 * BLOCKS + NARROWS
+WR = CR + 1
 
 
 def exchange_kernel(
     gs, gn, rs, rn, cs, cn,
     ts, tn, rowf, colfs, colfn, cscs, cscn,
     vs, vn, vrs, vrn, vcs, vcn, part, rb,
-    rows_buf, c_out, w_out, cz, cy, wz, wy, ag, sz, sn,
+    rows_buf, c_out, w_out, cz, cy, wz, wy, own, ag, sx,
     load_sem, send_sem, recv_sem,
 ):
     z, y = lax.axis_index("wide_0"), lax.axis_index("wide_1")
     x, core = lax.axis_index("narrow_0"), lax.axis_index("narrow_1")
+    me = lax.rem(z + OFFSET, 8)
+    is_owner = me < OWNERS
 
     def on_z(d):
         return {"wide_0": lax.rem(z + d, 8)}
@@ -45,22 +54,61 @@
     loads.append(pltpu.make_async_copy(gn, vn, load_sem.at[4]))
     for i, (a, b) in enumerate(((rs, vrs), (rn, vrn), (cs, vcs), (cn, vcn))):
         loads.append(pltpu.make_async_copy(a, b, load_sem.at[5 + i]))
+
     for c in loads:
         c.start()
 
     barrier = pltpu.get_barrier_semaphore()
     for d in FAR_FIRST:
-        for peer in (on_z(d), on_y(d), on_narrow(d)):
-            pl.semaphore_signal(barrier, inc=1, device_id=peer, device_id_type=MESH)
-
-    def send(kind, d, src, dst, peer):
-        c = pltpu.make_async_remote_copy(
-            src_ref=src, dst_ref=dst, send_sem=send_sem.at[kind, d], recv_sem=recv_sem.at[kind, d],
-            device_id=peer, device_id_type=MESH)
-        c.start()
-        return c
-
-    started = []
+        pl.semaphore_signal(barrier, inc=1, device_id=on_narrow(d), device_id_type=MESH)
+
+    @pl.when(is_owner)
+    def _():
+        for d in FAR_FIRST:
+            pl.semaphore_signal(barrier, inc=1, device_id=on_z(d), device_id_type=MESH)
+        for d in FAR_FIRST:
+            pl.semaphore_signal(barrier, inc=1, device_id=on_y(d), device_id_type=MESH)
+
+    def send(kind, src, dst, peer):
+        pltpu.make_async_remote_copy(
+            src_ref=src, dst_ref=dst, send_sem=send_sem.at[kind], recv_sem=recv_sem.at[kind],
+            device_id=peer, device_id_type=MESH).start()
+
+    def drained(kind, ref):
+        pltpu.make_async_remote_copy(
+            src_ref=ref, dst_ref=ref, send_sem=send_sem.at[kind], recv_sem=recv_sem.at[kind],
+            device_id=on_z(1), device_id_type=MESH).wait_send()
+
+    def arrived(kind, ref):
+        pltpu.make_async_remote_copy(
+            src_ref=ref, dst_ref=ref, send_sem=send_sem.at[kind], recv_sem=recv_sem.at[kind],
+            device_id=on_z(1), device_id_type=MESH).wait_recv()
+
+    def to_owners(kind, out, buf):
+        for o in range(OWNERS):
+            at = (o - OFFSET) % 8
+            slot = lax.rem(at + 8 - z, 8)
+
+            @pl.when(z != at)
+            def _():
+                send(kind, out.at[o], buf.at[slot], {"wide_0": at})
+
+    def drained_owners(kind, out):
+        @pl.when(is_owner)
+        def _():
+            drained(kind, out.at[pl.ds(0, OWNERS - 1)])
+
+        if OWNERS < 8:
+            @pl.when(jnp.logical_not(is_owner))
+            def _():
+                drained(kind, out)
+
+    def total_of(buf, place):
+        total = None
+        for s in range(8):
+            piece = buf[lax.rem(place + 8 - s, 8)]
+            total = piece if total is None else total + piece
+        return total
 
     def column_sums(m, ref, width):
         blocks = width // 128
@@ -78,35 +126,40 @@
         acc = lax.fori_loop(0, 8, step, jnp.zeros((8, width), f32), unroll=True)
         return jnp.sum(acc, axis=0, keepdims=True)
 
+    def place_square(out, m, k, row):
+        r = (k % BLOCKS) * 4 + m
+        out[k // BLOCKS, r:r + 1, :] = row
+
+    def place_narrow(out, m, row):
+        for o in range(OWNERS):
+            for i in range(NARROWS):
+                if (o * NARROWS + i) % 4 == m:
+                    out[o, 4 * BLOCKS + i:4 * BLOCKS + i + 1, :] = row
+
     for m in range(4):
         loads[m].wait()
         total = column_sums(m, vs.at[m], 1024)
         for k in range(8):
-            c_out[k, m:m + 1, :] = total[:, k * 128:(k + 1) * 128]
+            place_square(c_out, m, k, total[:, k * 128:(k + 1) * 128])
     loads[4].wait()
     for m in range(4):
-        total = column_sums(4 + m, vn.at[m], 128)
-        c_out[m, 4:5, :] = total
-        c_out[m + 4, 4:5, :] = total
+        place_narrow(c_out, m, column_sums(4 + m, vn.at[m], 128))
     for m in range(8):
         rows_buf[0, m:m + 1, :] = jnp.sum(part[m].T, axis=0, keepdims=True)
-
-    pl.semaphore_wait(barrier, 21)
-
-    row_copies = [send(ROWS, d, rows_buf.at[0], rows_buf.at[d], on_narrow(d)) for d in FAR_FIRST]
-    cz[0] = c_out[z]
-    cz_copies = [send(CZ, d, c_out.at[lax.rem(z + d, 8)], cz.at[d], on_z(d)) for d in FAR_FIRST]
-    started += row_copies + cz_copies
-
     for c in loads[5:]:
         c.wait()
 
-    for c in row_copies:
-        c.wait_recv()
+    pl.semaphore_wait(barrier, jnp.where(is_owner, 7 + OWNERS - 1 + 7, 7 + OWNERS))
+
+    for d in FAR_FIRST:
+        send(ROWS, rows_buf.at[0], rows_buf.at[d], on_narrow(d))
+    to_owners(CZ, c_out, cz)
+
+    arrived(ROWS, rows_buf.at[pl.ds(1, 7)])
     rowsum = None
-    for sx in range(4):
-        for sc in range(2):
-            slot = lax.rem(x + 4 - sx, 4) * 2 + lax.rem(core + sc, 2)
+    for s_x in range(4):
+        for s_c in range(2):
+            slot = lax.rem(x + 4 - s_x, 4) * 2 + lax.rem(core + s_c, 2)
             piece = rows_buf[slot]
             rowsum = piece if rowsum is None else rowsum + piece
     sub = lax.broadcasted_iota(jnp.int32, (8, 128), 0)
@@ -119,8 +172,8 @@
         rb[m] = jnp.broadcast_to(inverse[m:m + 1, :], (128, 128)).T
     totals = jnp.sum(factor, axis=1, keepdims=True)
     totals = jnp.sum(jnp.where(lane == sub, totals, 0.0), axis=0, keepdims=True)
-    for k in range(8):
-        w_out[k, 5:6, :] = totals
+    for o in range(OWNERS):
+        w_out[o, CR:CR + 1, :] = totals
 
     def weighted_sums(m, ref, out, width):
         blocks = width // 128
@@ -143,79 +196,105 @@
     for m in range(4):
         total = weighted_sums(m, vs.at[m], ts.at[m], 1024)
         for k in range(8):
-            w_out[k, m:m + 1, :] = total[k]
-    for m in range(4):
-        total = weighted_sums(4 + m, vn.at[m], tn.at[m], 128)[0]
-        w_out[m, 4:5, :] = total
-        w_out[m + 4, 4:5, :] = total
-
-    wz[0] = w_out[z]
-    wz_copies = [send(WZ, d, w_out.at[lax.rem(z + d, 8)], wz.at[d], on_z(d)) for d in FAR_FIRST]
-    started += wz_copies
-
-    def gathered(buf, me, copies):
-        for c in copies:
-            c.wait_recv()
-        total = None
-        for s in range(8):
-            piece = buf[lax.rem(me + 8 - s, 8)]
-            total = piece if total is None else total + piece
-        return total
-
-    cy[0] = gathered(cz, z, cz_copies)
-    cy_copies = [send(CY, d, cy.at[0], cy.at[d], on_y(d)) for d in FAR_FIRST]
-    started += cy_copies
-
-    wy[0] = gathered(wz, z, wz_copies)
-    wy_copies = [send(WY, d, wy.at[0], wy.at[d], on_y(d)) for d in FAR_FIRST]
-    started += wy_copies
-
-    colsum = gathered(cy, y, cy_copies)
-    state = vcs[:, pl.ds(pl.multiple_of(z * 128, 128), 128)]
-    ag[0, 0:4, :] = decay_rate * state + (1.0 - decay_rate) * (colsum[0:4] / 8192 + epsilon_square)
-    ag[0, 4:5, :] = (decay_rate * vcn[pl.ds(lax.rem(z, 4), 1), :]
-                     + (1.0 - decay_rate) * (colsum[4:5] / 8192 + epsilon_square))
-    ag_copies = [send(AG, d, ag.at[0], ag.at[d], on_z(d)) for d in FAR_FIRST]
-    started += ag_copies
-    own = ag[0]
-
-    weighted = gathered(wy, y, wy_copies)
-    share = jnp.sum(weighted[0:5] / own, axis=1, keepdims=True)
-    sub5, lane5 = sub[0:5], lane[0:5]
-    target = jnp.where(sub5 == 4, 4 + z, sub5)
-    share = jnp.sum(jnp.where(lane5 == target, share, 0.0), axis=0, keepdims=True)
-    sz[0] = share
-    sz_copies = [send(SZ, d, sz.at[0], sz.at[d], on_z(d)) for d in FAR_FIRST]
-    started += sz_copies
-
-    for c in ag_copies:
-        c.wait_recv()
-    for s in range(8):
-        piece = ag[lax.rem(z + 8 - s, 8)]
-        colfs[:, s * 128:(s + 1) * 128] = piece[0:4]
-        if s < 4:
-            colfn[s:s + 1, :] = piece[4:5]
+            place_square(w_out, m, k, total[k])
+    for m in range(4):
+        place_narrow(w_out, m, weighted_sums(4 + m, vn.at[m], tn.at[m], 128)[0])
+    to_owners(WZ, w_out, wz)
+
+    @pl.when(is_owner)
+    def _():
+        cz[0] = c_out[me]
+        wz[0] = w_out[me]
+        arrived(CZ, cz.at[pl.ds(1, 7)])
+        cy[0] = total_of(cz, z)
+        for d in FAR_FIRST:
+            send(CY, cy.at[0], cy.at[d], on_y(d))
+        arrived(WZ, wz.at[pl.ds(1, 7)])
+        wy[0] = total_of(wz, z)
+        for d in FAR_FIRST:
+            send(WY, wy.at[0], wy.at[d], on_y(d))
+
+        arrived(CY, cy.at[pl.ds(1, 7)])
+        colsum = total_of(cy, y) / 8192 + epsilon_square
+        for b in range(BLOCKS):
+            start = pl.multiple_of((me * BLOCKS + b) * 128, 128)
+            own[0, 4 * b:4 * b + 4, :] = (
+                decay_rate * vcs[:, pl.ds(start, 128)] + (1.0 - decay_rate) * colsum[4 * b:4 * b + 4])
+        for i in range(NARROWS):
+            r = 4 * BLOCKS + i
+            own[0, r:r + 1, :] = (
+                decay_rate * vcn[pl.ds(lax.rem(me * NARROWS + i, 4), 1), :]
+                + (1.0 - decay_rate) * colsum[r:r + 1])
+        for d in FAR_FIRST:
+            send(AG, own.at[0], ag.at[me], on_z(d))
+        colfactor = own[0]
+        ag[me] = colfactor
+
+        arrived(WY, wy.at[pl.ds(1, 7)])
+        weighted = total_of(wy, y)
+        share = jnp.sum(weighted[0:CR] / colfactor, axis=1, keepdims=True)
+        subc = lax.broadcasted_iota(jnp.int32, (CR, 128), 0)
+        lanec = lax.broadcasted_iota(jnp.int32, (CR, 128), 1)
+        target = jnp.where(subc >= 4 * BLOCKS, subc - 4 * BLOCKS + 4 + me * NARROWS, lax.rem(subc, 4))
+        share = jnp.sum(jnp.where(lanec == target, share, 0.0), axis=0, keepdims=True)
+        means = jnp.where(me == 0, pltpu.roll(weighted[CR:CR + 1], 16, 1), 0.0)
+        sx[me * 8] = share + means
+        for dz in (0,) + FAR_FIRST[::-1]:
+            for d in FAR_FIRST + (0,):
+                if (dz, d) != (0, 0):
+                    peer = {**on_z(dz), **on_narrow(d)}
+                    send(SX, sx.at[me * 8], sx.at[me * 8 + d], peer)
+
+    @pl.when(is_owner)
+    def _():
+        arrived(AG, ag.at[pl.ds(0, OWNERS - 1)])
+
+    if OWNERS < 8:
+        @pl.when(jnp.logical_not(is_owner))
+        def _():
+            arrived(AG, ag)
+
+    for o in range(OWNERS):
+        piece = ag[o]
+        for b in range(BLOCKS):
+            k = o * BLOCKS + b
+            colfs[:, k * 128:(k + 1) * 128] = piece[4 * b:4 * b + 4]
+        for i in range(NARROWS):
+            if o * NARROWS + i < 4:
+                colfn[o * NARROWS + i:o * NARROWS + i + 1, :] = piece[4 * BLOCKS + i:4 * BLOCKS + i + 1]
     inv_s, inv_n = lax.rsqrt(colfs[...]), lax.rsqrt(colfn[...])
 
-    sn[0] = gathered(sz, z, sz_copies)
-    sn_copies = [send(SN, d, sn.at[0], sn.at[d], on_narrow(d)) for d in FAR_FIRST]
-    started += sn_copies
-    for c in sn_copies:
-        c.wait_recv()
-    norm = sn[0]
-    for d in range(1, 8):
-        norm = norm + sn[d]
+    @pl.when(is_owner)
+    def _():
+        arrived(SX, sx.at[pl.ds(0, 8 * OWNERS - 1)])
+
+    if OWNERS < 8:
+        @pl.when(jnp.logical_not(is_owner))
+        def _():
+            arrived(SX, sx)
+
+    norm = sx[0]
+    for i in range(1, 8 * OWNERS):
+        norm = norm + sx[i]
     lane1 = lane[0:1]
     entries = jnp.where(lane1 < 4, 8192.0 * 8192.0, 8192.0 * 1024.0)
-    row_mean = weighted[5:6] / 8192
+    row_mean = pltpu.roll(norm, 128 - 16, 1) / (8 * 8192)
     spread = jnp.sqrt(row_mean * norm / entries)
     scale = jnp.sqrt(row_mean) / jnp.maximum(1.0, spread / clip_limit)
     scale = jnp.sum(jnp.where(lane == sub, jnp.broadcast_to(scale, (8, 128)), 0.0), axis=1, keepdims=True)
     cscs[...] = inv_s * scale[0:4]
     cscn[...] = inv_n * scale[4:8]
 
-    for c in started:
-        c.wait_send()
+    drained(ROWS, rows_buf.at[pl.ds(1, 7)])
+    drained_owners(CZ, c_out)
+    drained_owners(WZ, w_out)
+
+    @pl.when(is_owner)
+    def _():
+        drained(CY, cy.at[pl.ds(1, 7)])
+        drained(WY, wy.at[pl.ds(1, 7)])
+        drained(AG, cy.at[pl.ds(1, 7)])
+        drained(SX, part.at[0, pl.ds(0, 63)])
 
 
 def output_kernel(
@@ -268,13 +347,14 @@
             V((4, 128), f32), V((4, 128), f32), V((4, 1024), f32), V((4, 128), f32),
             V((8, 128, 128), f32), V((8, 128, 128), f32),
             V((8, 8, 128), f32),
-            V((8, 5, 128), f32), V((8, 6, 128), f32),
-            V((8, 5, 128), f32), V((8, 5, 128), f32),
-            V((8, 6, 128), f32), V((8, 6, 128), f32),
-            V((8, 5, 128), f32), V((8, 1, 128), f32), V((8, 1, 128), f32),
+            V((OWNERS, CR, 128), f32), V((OWNERS, WR, 128), f32),
+            V((8, CR, 128), f32), V((8, CR, 128), f32),
+            V((8, WR, 128), f32), V((8, WR, 128), f32),
+            V((1, CR, 128), f32), V((OWNERS, CR, 128), f32),
+            V((8 * OWNERS, 1, 128), f32),
             pltpu.SemaphoreType.DMA((9,)),
-            pltpu.SemaphoreType.DMA((8, 8)),
-            pltpu.SemaphoreType.DMA((8, 8)),
+            pltpu.SemaphoreType.DMA((7,)),
+            pltpu.SemaphoreType.DMA((7,)),
         ],
         compiler_params=pltpu.CompilerParams(
             collective_id=0, has_side_effects=True, vmem_limit_bytes=24 * 2**20),

time: 39 us -> 35.4 us (0.908)
  Pallas kernels: 38.2 us -> 34.6 us
    pallas_call x1, Pallas kernels: 36.7 us -> 33.1 us  [per_device(): pl.pallas_call(exchange_kernel, out_shape=[jax.ShapeDtypeStruct((4, 128,...]
where the time goes in v2:
time: 35.4 us; the launch traced here: 35.3 us
  Pallas kernels  34.6 us (98%)
  between operations  0.64 us (2%)
    pallas_call x1, Pallas kernels, per_device(): pl.pallas_call(exchange_kernel, out_shape=[jax.ShapeDtypeStruct((4, 128,...  33.1 us
    pallas_call x1, Pallas kernels, per_device(): pl.pallas_call(output_kernel, out_shape=[jax.ShapeDtypeStruct((4, 128, 10...  1.51 us

profile of v2, /device:TPU:1, one launch (start us, length us, event | category | flops | bytes accessed | tf_op | source)
XLA Modules:
  0.0 35.3 jit_solution(4635484040346582533)
XLA Ops:
  0.6 33.1 %exchange.1 = (f32[4,128,1024]{2,1,0:T(8,128)S(1)}, f32[4,128,128]{2,1,0:T(8,128)S(1)}, f32[8,128]{1,0:T(8,128)S(1)}, f32[4,1024]{1,0:T(4,128)S(1)}, f32[4,128]{...) custom-call(bf16[4,128,1024]{2,1,0:T(8,128)(2,1)} %gs.1, bf16[4,128,128]{2,1,0:T(8,128)(2,1)} %gn.1, ...), custom_call_target="tpu_custom_call" | custom-call | tf_op jit(solution)/shard_map/exchange/pallas_call | solution.py:335
  33.7 1.5 %output.1 = (f32[4,128,1024]{2,1,0:T(8,128)}, f32[4,128,128]{2,1,0:T(8,128)}, f32[4,128]{1,0:T(4,128)}, f32[4,1024]{1,0:T(4,128)}, f32[4,128]{1,0:T(4,128)}, /*index=5*/f32[4,128]{1,0:T(4,128)}) custom-call(f32[4,128,1024]{2,1,0:T(8,128)S(1)} %get-tuple-element.13.ts, f32[4,128,128]{2,1,0:T(8,128)S(1)} %get-tuple-element.14.tn, ...), custom_call_target="tpu_custom_call" | custom-call | tf_op jit(solution)/shard_map/output/pallas_call | solution.py:364

commit v3 on v2

--- a/solution.py
+++ b/solution.py
@@ -25,8 +25,11 @@
 OFFSET = 0
 BLOCKS = 8 // OWNERS
 NARROWS = max(1, 4 // OWNERS)
-CR = 4 * BLOCKS + NARROWS
+SQ = 4 * BLOCKS
+CR = SQ + NARROWS
 WR = CR + 1
+CR2 = 2 * CR
+WR2 = CR2 + 1
 
 
 def exchange_kernel(
@@ -39,33 +42,32 @@
     z, y = lax.axis_index("wide_0"), lax.axis_index("wide_1")
     x, core = lax.axis_index("narrow_0"), lax.axis_index("narrow_1")
     me = lax.rem(z + OFFSET, 8)
-    is_owner = me < OWNERS
-
-    def on_z(d):
-        return {"wide_0": lax.rem(z + d, 8)}
+    on_plane = me < OWNERS
+    is_owner = jnp.logical_and(on_plane, core == 1)
 
     def on_y(d):
         return {"wide_1": lax.rem(y + d, 8)}
 
     def on_narrow(d):
         return {"narrow_0": lax.rem(x + d // 2, 4), "narrow_1": lax.rem(core + d % 2, 2)}
+
+    barrier = pltpu.get_barrier_semaphore()
+    for d in FAR_FIRST:
+        pl.semaphore_signal(barrier, inc=1, device_id=on_narrow(d), device_id_type=MESH)
 
     loads = [pltpu.make_async_copy(gs.at[m], vs.at[m], load_sem.at[m]) for m in range(4)]
     loads.append(pltpu.make_async_copy(gn, vn, load_sem.at[4]))
     for i, (a, b) in enumerate(((rs, vrs), (rn, vrn), (cs, vcs), (cn, vcn))):
         loads.append(pltpu.make_async_copy(a, b, load_sem.at[5 + i]))
-
     for c in loads:
         c.start()
-
-    barrier = pltpu.get_barrier_semaphore()
-    for d in FAR_FIRST:
-        pl.semaphore_signal(barrier, inc=1, device_id=on_narrow(d), device_id_type=MESH)
 
     @pl.when(is_owner)
     def _():
         for d in FAR_FIRST:
-            pl.semaphore_signal(barrier, inc=1, device_id=on_z(d), device_id_type=MESH)
+            for c in range(2):
+                peer = {"wide_0": lax.rem(z + d, 8), "narrow_1": c}
+                pl.semaphore_signal(barrier, inc=1, device_id=peer, device_id_type=MESH)
         for d in FAR_FIRST:
             pl.semaphore_signal(barrier, inc=1, device_id=on_y(d), device_id_type=MESH)
 
@@ -77,38 +79,24 @@
     def drained(kind, ref):
         pltpu.make_async_remote_copy(
             src_ref=ref, dst_ref=ref, send_sem=send_sem.at[kind], recv_sem=recv_sem.at[kind],
-            device_id=on_z(1), device_id_type=MESH).wait_send()
+            device_id=on_y(1), device_id_type=MESH).wait_send()
 
     def arrived(kind, ref):
         pltpu.make_async_remote_copy(
             src_ref=ref, dst_ref=ref, send_sem=send_sem.at[kind], recv_sem=recv_sem.at[kind],
-            device_id=on_z(1), device_id_type=MESH).wait_recv()
+            device_id=on_y(1), device_id_type=MESH).wait_recv()
+
+    def if_owner(then, otherwise):
+        pl.when(is_owner)(then)
+        pl.when(jnp.logical_not(is_owner))(otherwise)
 
     def to_owners(kind, out, buf):
         for o in range(OWNERS):
             at = (o - OFFSET) % 8
-            slot = lax.rem(at + 8 - z, 8)
-
-            @pl.when(z != at)
+
+            @pl.when(jnp.logical_or(z != at, core == 0))
             def _():
-                send(kind, out.at[o], buf.at[slot], {"wide_0": at})
-
-    def drained_owners(kind, out):
-        @pl.when(is_owner)
-        def _():
-            drained(kind, out.at[pl.ds(0, OWNERS - 1)])
-
-        if OWNERS < 8:
-            @pl.when(jnp.logical_not(is_owner))
-            def _():
-                drained(kind, out)
-
-    def total_of(buf, place):
-        total = None
-        for s in range(8):
-            piece = buf[lax.rem(place + 8 - s, 8)]
-            total = piece if total is None else total + piece
-        return total
+                send(kind, out.at[o], buf.at[z * 2 + core], {"wide_0": at, "narrow_1": 1})
 
     def column_sums(m, ref, width):
         blocks = width // 128
@@ -134,22 +122,25 @@
         for o in range(OWNERS):
             for i in range(NARROWS):
                 if (o * NARROWS + i) % 4 == m:
-                    out[o, 4 * BLOCKS + i:4 * BLOCKS + i + 1, :] = row
-
+                    out[o, SQ + i:SQ + i + 1, :] = row
+
+    old = decay_rate / (1.0 - decay_rate) * 8192 / 64
     for m in range(4):
         loads[m].wait()
-        total = column_sums(m, vs.at[m], 1024)
+        if m == 0:
+            for c in loads[5:]:
+                c.wait()
+        total = column_sums(m, vs.at[m], 1024) + old * vcs[m:m + 1, :]
         for k in range(8):
             place_square(c_out, m, k, total[:, k * 128:(k + 1) * 128])
     loads[4].wait()
     for m in range(4):
-        place_narrow(c_out, m, column_sums(4 + m, vn.at[m], 128))
+        place_narrow(c_out, m, column_sums(4 + m, vn.at[m], 128) + old * vcn[m:m + 1, :])
     for m in range(8):
         rows_buf[0, m:m + 1, :] = jnp.sum(part[m].T, axis=0, keepdims=True)
-    for c in loads[5:]:
-        c.wait()
-
-    pl.semaphore_wait(barrier, jnp.where(is_owner, 7 + OWNERS - 1 + 7, 7 + OWNERS))
+
+    others = jnp.where(on_plane, OWNERS - 1, OWNERS)
+    pl.semaphore_wait(barrier, 7 + others + jnp.where(is_owner, 7, 0))
 
     for d in FAR_FIRST:
         send(ROWS, rows_buf.at[0], rows_buf.at[d], on_narrow(d))
@@ -201,59 +192,65 @@
         place_narrow(w_out, m, weighted_sums(4 + m, vn.at[m], tn.at[m], 128)[0])
     to_owners(WZ, w_out, wz)
 
+    def over_z(kind, out, buf, into):
+        arrived(kind, buf.at[pl.ds(0, 15)])
+        for c in range(2):
+            total = None
+            for s in range(8):
+                piece = jnp.where(jnp.logical_and(z == s, c == 1), out[me], buf[2 * s + c])
+                total = piece if total is None else total + piece
+            into[y, SQ * c:SQ * c + SQ, :] = total[0:SQ]
+            into[y, 2 * SQ + NARROWS * c:2 * SQ + NARROWS * (c + 1), :] = total[SQ:CR]
+        if kind == WZ:
+            into[y, CR2:WR2, :] = total[CR:WR]
+
+    def over_y(kind, buf):
+        arrived(kind, buf.at[pl.ds(0, 7)])
+        total = buf[0]
+        for s in range(1, 8):
+            total = total + buf[s]
+        return total
+
     @pl.when(is_owner)
     def _():
-        cz[0] = c_out[me]
-        wz[0] = w_out[me]
-        arrived(CZ, cz.at[pl.ds(1, 7)])
-        cy[0] = total_of(cz, z)
+        over_z(CZ, c_out, cz, cy)
         for d in FAR_FIRST:
-            send(CY, cy.at[0], cy.at[d], on_y(d))
-        arrived(WZ, wz.at[pl.ds(1, 7)])
-        wy[0] = total_of(wz, z)
+            send(CY, cy.at[y], cy.at[y], on_y(d))
+        over_z(WZ, w_out, wz, wy)
         for d in FAR_FIRST:
-            send(WY, wy.at[0], wy.at[d], on_y(d))
-
-        arrived(CY, cy.at[pl.ds(1, 7)])
-        colsum = total_of(cy, y) / 8192 + epsilon_square
-        for b in range(BLOCKS):
-            start = pl.multiple_of((me * BLOCKS + b) * 128, 128)
-            own[0, 4 * b:4 * b + 4, :] = (
-                decay_rate * vcs[:, pl.ds(start, 128)] + (1.0 - decay_rate) * colsum[4 * b:4 * b + 4])
-        for i in range(NARROWS):
-            r = 4 * BLOCKS + i
-            own[0, r:r + 1, :] = (
-                decay_rate * vcn[pl.ds(lax.rem(me * NARROWS + i, 4), 1), :]
-                + (1.0 - decay_rate) * colsum[r:r + 1])
-        for d in FAR_FIRST:
-            send(AG, own.at[0], ag.at[me], on_z(d))
-        colfactor = own[0]
-        ag[me] = colfactor
-
-        arrived(WY, wy.at[pl.ds(1, 7)])
-        weighted = total_of(wy, y)
-        share = jnp.sum(weighted[0:CR] / colfactor, axis=1, keepdims=True)
-        subc = lax.broadcasted_iota(jnp.int32, (CR, 128), 0)
-        lanec = lax.broadcasted_iota(jnp.int32, (CR, 128), 1)
-        target = jnp.where(subc >= 4 * BLOCKS, subc - 4 * BLOCKS + 4 + me * NARROWS, lax.rem(subc, 4))
-        share = jnp.sum(jnp.where(lanec == target, share, 0.0), axis=0, keepdims=True)
-        means = jnp.where(me == 0, pltpu.roll(weighted[CR:CR + 1], 16, 1), 0.0)
-        sx[me * 8] = share + means
-        for dz in (0,) + FAR_FIRST[::-1]:
-            for d in FAR_FIRST + (0,):
-                if (dz, d) != (0, 0):
-                    peer = {**on_z(dz), **on_narrow(d)}
-                    send(SX, sx.at[me * 8], sx.at[me * 8 + d], peer)
-
-    @pl.when(is_owner)
-    def _():
-        arrived(AG, ag.at[pl.ds(0, OWNERS - 1)])
-
-    if OWNERS < 8:
-        @pl.when(jnp.logical_not(is_owner))
-        def _():
-            arrived(AG, ag)
-
+            send(WY, wy.at[y], wy.at[y], on_y(d))
+
+        colfactor = (1.0 - decay_rate) * (over_y(CY, cy) / 8192 + epsilon_square)
+        for c in range(2):
+            own[c, 0:SQ, :] = colfactor[SQ * c:SQ * c + SQ]
+            own[c, SQ:CR, :] = colfactor[2 * SQ + NARROWS * c:2 * SQ + NARROWS * (c + 1)]
+        for d in FAR_FIRST + (0,):
+            for c in range(2):
+                if (d, c) != (0, 1):
+                    send(AG, own.at[c], ag.at[me], {"wide_0": lax.rem(z + d, 8), "narrow_1": c})
+        ag[me] = own[1]
+
+        weighted = over_y(WY, wy)
+        share = jnp.sum(weighted[0:CR2] / colfactor, axis=1, keepdims=True)
+        subc = lax.broadcasted_iota(jnp.int32, (CR2, 128), 0)
+        lanec = lax.broadcasted_iota(jnp.int32, (CR2, 128), 1)
+        narrow = 4 + me * NARROWS + lax.rem(subc - 2 * SQ, NARROWS)
+        target = jnp.where(subc >= 2 * SQ, narrow, lax.rem(subc, 4))
+        sx[me * 4 + x, 0:1, :] = jnp.sum(jnp.where(lanec == target, share, 0.0), axis=0, keepdims=True)
+        sx[me * 4 + x, 1:2, :] = weighted[CR2:WR2]
+        mine = sx.at[me * 4 + x]
+        for t_z in (0, 1, 7, 2, 6, 3, 5, 4):
+            for t_x in (0, 1, 3, 2):
+                for t_c in (1, 0):
+                    peer = {"wide_0": t_z, "narrow_0": t_x, "narrow_1": t_c}
+                    if t_c == 0:
+                        send(SX, mine, mine, peer)
+                    else:
+                        @pl.when(jnp.logical_or(z != t_z, x != t_x))
+                        def _():
+                            send(SX, mine, mine, peer)
+
+    if_owner(lambda: arrived(AG, ag.at[pl.ds(0, OWNERS - 1)]), lambda: arrived(AG, ag))
     for o in range(OWNERS):
         piece = ag[o]
         for b in range(BLOCKS):
@@ -261,40 +258,36 @@
             colfs[:, k * 128:(k + 1) * 128] = piece[4 * b:4 * b + 4]
         for i in range(NARROWS):
             if o * NARROWS + i < 4:
-                colfn[o * NARROWS + i:o * NARROWS + i + 1, :] = piece[4 * BLOCKS + i:4 * BLOCKS + i + 1]
+                colfn[o * NARROWS + i:o * NARROWS + i + 1, :] = piece[SQ + i:SQ + i + 1]
     inv_s, inv_n = lax.rsqrt(colfs[...]), lax.rsqrt(colfn[...])
 
-    @pl.when(is_owner)
-    def _():
-        arrived(SX, sx.at[pl.ds(0, 8 * OWNERS - 1)])
-
-    if OWNERS < 8:
-        @pl.when(jnp.logical_not(is_owner))
-        def _():
-            arrived(SX, sx)
-
-    norm = sx[0]
-    for i in range(1, 8 * OWNERS):
-        norm = norm + sx[i]
-    lane1 = lane[0:1]
-    entries = jnp.where(lane1 < 4, 8192.0 * 8192.0, 8192.0 * 1024.0)
-    row_mean = pltpu.roll(norm, 128 - 16, 1) / (8 * 8192)
-    spread = jnp.sqrt(row_mean * norm / entries)
+    if_owner(lambda: arrived(SX, sx.at[pl.ds(0, 4 * OWNERS - 1)]), lambda: arrived(SX, sx))
+    pair = sx[0]
+    for i in range(1, 4 * OWNERS):
+        pair = pair + sx[i]
+    entries = jnp.where(lane[0:1] < 4, 8192.0 * 8192.0, 8192.0 * 1024.0)
+    row_mean = pair[1:2] / (4 * OWNERS * 8192)
+    spread = jnp.sqrt(row_mean * pair[0:1] / entries)
     scale = jnp.sqrt(row_mean) / jnp.maximum(1.0, spread / clip_limit)
     scale = jnp.sum(jnp.where(lane == sub, jnp.broadcast_to(scale, (8, 128)), 0.0), axis=1, keepdims=True)
     cscs[...] = inv_s * scale[0:4]
     cscn[...] = inv_n * scale[4:8]
 
     drained(ROWS, rows_buf.at[pl.ds(1, 7)])
-    drained_owners(CZ, c_out)
-    drained_owners(WZ, w_out)
-
-    @pl.when(is_owner)
-    def _():
-        drained(CY, cy.at[pl.ds(1, 7)])
-        drained(WY, wy.at[pl.ds(1, 7)])
-        drained(AG, cy.at[pl.ds(1, 7)])
-        drained(SX, part.at[0, pl.ds(0, 63)])
+
+    def drain_owner():
+        drained(CZ, c_out.at[pl.ds(0, OWNERS - 1)])
+        drained(WZ, w_out.at[pl.ds(0, OWNERS - 1)])
+        drained(CY, cy.at[pl.ds(0, 7)])
+        drained(WY, wy.at[pl.ds(0, 7)])
+        drained(AG, cz.at[pl.ds(0, 15)])
+        drained(SX, part.at[0, pl.ds(0, 126)])
+
+    def drain_other():
+        drained(CZ, c_out)
+        drained(WZ, w_out)
+
+    if_owner(drain_owner, drain_other)
 
 
 def output_kernel(
@@ -348,10 +341,10 @@
             V((8, 128, 128), f32), V((8, 128, 128), f32),
             V((8, 8, 128), f32),
             V((OWNERS, CR, 128), f32), V((OWNERS, WR, 128), f32),
-            V((8, CR, 128), f32), V((8, CR, 128), f32),
-            V((8, WR, 128), f32), V((8, WR, 128), f32),
-            V((1, CR, 128), f32), V((OWNERS, CR, 128), f32),
-            V((8 * OWNERS, 1, 128), f32),
+            V((16, CR, 128), f32), V((8, CR2, 128), f32),
+            V((16, WR, 128), f32), V((8, WR2, 128), f32),
+            V((2, CR, 128), f32), V((OWNERS, CR, 128), f32),
+            V((4 * OWNERS, 2, 128), f32),
             pltpu.SemaphoreType.DMA((9,)),
             pltpu.SemaphoreType.DMA((7,)),
             pltpu.SemaphoreType.DMA((7,)),

time: 35.4 us -> 33.6 us (0.949)
  Pallas kernels: 34.6 us -> 32.9 us
    pallas_call x1, Pallas kernels: 33.1 us -> 31.3 us  [per_device(): pl.pallas_call(exchange_kernel, out_shape=[jax.ShapeDtypeStruct((4, 128,...]
where the time goes in v3:
time: 33.6 us; the launch traced here: 33.5 us
  Pallas kernels  32.9 us (98%)
  between operations  0.64 us (2%)
    pallas_call x1, Pallas kernels, per_device(): pl.pallas_call(exchange_kernel, out_shape=[jax.ShapeDtypeStruct((4, 128,...  31.3 us
    pallas_call x1, Pallas kernels, per_device(): pl.pallas_call(output_kernel, out_shape=[jax.ShapeDtypeStruct((4, 128, 10...  1.51 us

profile of v3, /device:TPU:1, one launch (start us, length us, event | category | flops | bytes accessed | tf_op | source)
XLA Modules:
  0.0 33.5 jit_solution(7881165544156285036)
XLA Ops:
  0.6 31.3 %exchange.1 = (f32[4,128,1024]{2,1,0:T(8,128)S(1)}, f32[4,128,128]{2,1,0:T(8,128)S(1)}, f32[8,128]{1,0:T(8,128)S(1)}, f32[4,1024]{1,0:T(4,128)S(1)}, f32[4,128]{...) custom-call(bf16[4,128,1024]{2,1,0:T(8,128)(2,1)} %gs.1, bf16[4,128,128]{2,1,0:T(8,128)(2,1)} %gn.1, ...), custom_call_target="tpu_custom_call" | custom-call | tf_op jit(solution)/shard_map/exchange/pallas_call | solution.py:328
  32.0 1.5 %output.1 = (f32[4,128,1024]{2,1,0:T(8,128)}, f32[4,128,128]{2,1,0:T(8,128)}, f32[4,128]{1,0:T(4,128)}, f32[4,1024]{1,0:T(4,128)}, f32[4,128]{1,0:T(4,128)}, /*index=5*/f32[4,128]{1,0:T(4,128)}) custom-call(f32[4,128,1024]{2,1,0:T(8,128)S(1)} %get-tuple-element.13.ts, f32[4,128,128]{2,1,0:T(8,128)S(1)} %get-tuple-element.14.tn, ...), custom_call_target="tpu_custom_call" | custom-call | tf_op jit(solution)/shard_map/output/pallas_call | solution.py:357

commit v4 on v3

--- a/solution.py
+++ b/solution.py
@@ -18,10 +18,10 @@
 
 f32 = jnp.float32
 
-ROWS, CZ, CY, WZ, WY, AG, SX = range(7)
+ROWS, CZ, CY, WZ, AG, TX, SX = range(7)
 FAR_FIRST = (4, 3, 5, 2, 6, 1, 7)
 
-OWNERS = 4
+OWNERS = 2
 OFFSET = 0
 BLOCKS = 8 // OWNERS
 NARROWS = max(1, 4 // OWNERS)
@@ -30,13 +30,16 @@
 WR = CR + 1
 CR2 = 2 * CR
 WR2 = CR2 + 1
+ROOT_ZS = (0, 1)
+ROOTS = [(t_z, t_y, t_x) for t_y in (0, 1, 2, 3, 7, 4, 6, 5) for t_z in ROOT_ZS for t_x in (0, 1, 3, 2)]
+SERVED = range(4) if len(ROOT_ZS) == 2 else (0, 1, 7, 2, 6, 3, 5, 4)
 
 
 def exchange_kernel(
     gs, gn, rs, rn, cs, cn,
     ts, tn, rowf, colfs, colfn, cscs, cscn,
     vs, vn, vrs, vrn, vcs, vcn, part, rb,
-    rows_buf, c_out, w_out, cz, cy, wz, wy, own, ag, sx,
+    rows_buf, c_out, w_out, cz, cy, wz, w_all, own, ag, tx, sx,
     load_sem, send_sem, recv_sem,
 ):
     z, y = lax.axis_index("wide_0"), lax.axis_index("wide_1")
@@ -44,6 +47,7 @@
     me = lax.rem(z + OFFSET, 8)
     on_plane = me < OWNERS
     is_owner = jnp.logical_and(on_plane, core == 1)
+    is_root = jnp.logical_and(z < len(ROOT_ZS), core == 1)
 
     def on_y(d):
         return {"wide_1": lax.rem(y + d, 8)}
@@ -91,10 +95,12 @@
         pl.when(jnp.logical_not(is_owner))(otherwise)
 
     def to_owners(kind, out, buf):
-        for o in range(OWNERS):
-            at = (o - OFFSET) % 8
-
-            @pl.when(jnp.logical_or(z != at, core == 0))
+        for d in FAR_FIRST + (0,):
+            at = lax.rem(z + d, 8)
+            o = lax.rem(at + OFFSET, 8)
+            there = o < OWNERS
+
+            @pl.when(there if d else jnp.logical_and(there, core == 0))
             def _():
                 send(kind, out.at[o], buf.at[z * 2 + core], {"wide_0": at, "narrow_1": 1})
 
@@ -162,7 +168,7 @@
     for m in range(8):
         rb[m] = jnp.broadcast_to(inverse[m:m + 1, :], (128, 128)).T
     totals = jnp.sum(factor, axis=1, keepdims=True)
-    totals = jnp.sum(jnp.where(lane == sub, totals, 0.0), axis=0, keepdims=True)
+    totals = jnp.sum(jnp.where(lane == sub + 8, totals, 0.0), axis=0, keepdims=True)
     for o in range(OWNERS):
         w_out[o, CR:CR + 1, :] = totals
 
@@ -192,35 +198,28 @@
         place_narrow(w_out, m, weighted_sums(4 + m, vn.at[m], tn.at[m], 128)[0])
     to_owners(WZ, w_out, wz)
 
-    def over_z(kind, out, buf, into):
+    def over_z(kind, out, buf, into, slot):
         arrived(kind, buf.at[pl.ds(0, 15)])
         for c in range(2):
             total = None
             for s in range(8):
                 piece = jnp.where(jnp.logical_and(z == s, c == 1), out[me], buf[2 * s + c])
                 total = piece if total is None else total + piece
-            into[y, SQ * c:SQ * c + SQ, :] = total[0:SQ]
-            into[y, 2 * SQ + NARROWS * c:2 * SQ + NARROWS * (c + 1), :] = total[SQ:CR]
+            into[slot, SQ * c:SQ * c + SQ, :] = total[0:SQ]
+            into[slot, 2 * SQ + NARROWS * c:2 * SQ + NARROWS * (c + 1), :] = total[SQ:CR]
         if kind == WZ:
-            into[y, CR2:WR2, :] = total[CR:WR]
-
-    def over_y(kind, buf):
-        arrived(kind, buf.at[pl.ds(0, 7)])
-        total = buf[0]
-        for s in range(1, 8):
-            total = total + buf[s]
-        return total
+            into[slot, CR2:WR2, :] = total[CR:WR]
 
     @pl.when(is_owner)
     def _():
-        over_z(CZ, c_out, cz, cy)
+        over_z(CZ, c_out, cz, cy, y)
         for d in FAR_FIRST:
             send(CY, cy.at[y], cy.at[y], on_y(d))
-        over_z(WZ, w_out, wz, wy)
-        for d in FAR_FIRST:
-            send(WY, wy.at[y], wy.at[y], on_y(d))
-
-        colfactor = (1.0 - decay_rate) * (over_y(CY, cy) / 8192 + epsilon_square)
+        arrived(CY, cy.at[pl.ds(0, 7)])
+        colsum = cy[0]
+        for s in range(1, 8):
+            colsum = colsum + cy[s]
+        colfactor = (1.0 - decay_rate) * (colsum / 8192 + epsilon_square)
         for c in range(2):
             own[c, 0:SQ, :] = colfactor[SQ * c:SQ * c + SQ]
             own[c, SQ:CR, :] = colfactor[2 * SQ + NARROWS * c:2 * SQ + NARROWS * (c + 1)]
@@ -229,28 +228,29 @@
                 if (d, c) != (0, 1):
                     send(AG, own.at[c], ag.at[me], {"wide_0": lax.rem(z + d, 8), "narrow_1": c})
         ag[me] = own[1]
-
-        weighted = over_y(WY, wy)
-        share = jnp.sum(weighted[0:CR2] / colfactor, axis=1, keepdims=True)
+        inverse = 1.0 / colfactor
+
+        over_z(WZ, w_out, wz, w_all, 0)
+        weighted = w_all[0]
+        share = jnp.sum(weighted[0:CR2] * inverse, axis=1, keepdims=True)
         subc = lax.broadcasted_iota(jnp.int32, (CR2, 128), 0)
         lanec = lax.broadcasted_iota(jnp.int32, (CR2, 128), 1)
         narrow = 4 + me * NARROWS + lax.rem(subc - 2 * SQ, NARROWS)
         target = jnp.where(subc >= 2 * SQ, narrow, lax.rem(subc, 4))
-        sx[me * 4 + x, 0:1, :] = jnp.sum(jnp.where(lanec == target, share, 0.0), axis=0, keepdims=True)
-        sx[me * 4 + x, 1:2, :] = weighted[CR2:WR2]
-        mine = sx.at[me * 4 + x]
-        for t_z in (0, 1, 7, 2, 6, 3, 5, 4):
-            for t_x in (0, 1, 3, 2):
-                for t_c in (1, 0):
-                    peer = {"wide_0": t_z, "narrow_0": t_x, "narrow_1": t_c}
-                    if t_c == 0:
-                        send(SX, mine, mine, peer)
-                    else:
-                        @pl.when(jnp.logical_or(z != t_z, x != t_x))
-                        def _():
-                            send(SX, mine, mine, peer)
-
-    if_owner(lambda: arrived(AG, ag.at[pl.ds(0, OWNERS - 1)]), lambda: arrived(AG, ag))
+        slot = (me * 8 + y) * 4 + x
+        share = jnp.sum(jnp.where(lanec == target, share, 0.0), axis=0, keepdims=True)
+        tx[slot] = share + weighted[CR2:WR2]
+        mine = tx.at[slot]
+        for t_z, t_y, t_x in ROOTS:
+            @pl.when(jnp.logical_or(jnp.logical_or(z != t_z, y != t_y), x != t_x))
+            def _():
+                send(TX, mine, mine, {"wide_0": t_z, "wide_1": t_y, "narrow_0": t_x})
+
+    def owner_arrived():
+        if OWNERS > 1:
+            arrived(AG, ag.at[pl.ds(0, OWNERS - 1)])
+
+    if_owner(owner_arrived, lambda: arrived(AG, ag))
     for o in range(OWNERS):
         piece = ag[o]
         for b in range(BLOCKS):
@@ -261,27 +261,48 @@
                 colfn[o * NARROWS + i:o * NARROWS + i + 1, :] = piece[SQ + i:SQ + i + 1]
     inv_s, inv_n = lax.rsqrt(colfs[...]), lax.rsqrt(colfn[...])
 
-    if_owner(lambda: arrived(SX, sx.at[pl.ds(0, 4 * OWNERS - 1)]), lambda: arrived(SX, sx))
-    pair = sx[0]
-    for i in range(1, 4 * OWNERS):
-        pair = pair + sx[i]
-    entries = jnp.where(lane[0:1] < 4, 8192.0 * 8192.0, 8192.0 * 1024.0)
-    row_mean = pair[1:2] / (4 * OWNERS * 8192)
-    spread = jnp.sqrt(row_mean * pair[0:1] / entries)
-    scale = jnp.sqrt(row_mean) / jnp.maximum(1.0, spread / clip_limit)
-    scale = jnp.sum(jnp.where(lane == sub, jnp.broadcast_to(scale, (8, 128)), 0.0), axis=1, keepdims=True)
+    @pl.when(is_root)
+    def _():
+        arrived(TX, tx.at[pl.ds(0, 32 * OWNERS - 1)])
+        sums = [tx[i] for i in range(4)]
+        for i in range(4, 32 * OWNERS):
+            sums[i % 4] = sums[i % 4] + tx[i]
+        pair = (sums[0] + sums[1]) + (sums[2] + sums[3])
+        entries = jnp.where(lane[0:1] < 4, 8192.0 * 8192.0, 8192.0 * 1024.0)
+        row_mean = pltpu.roll(pair, 128 - 8, 1) / (4 * OWNERS * 8192)
+        spread = jnp.sqrt(row_mean * pair / entries)
+        sx[...] = jnp.sqrt(row_mean) / jnp.maximum(1.0, spread / clip_limit)
+        for i in SERVED:
+            for c in (1, 0):
+                if (i, c) != (0, 1):
+                    at = z + i if len(ROOT_ZS) == 1 else z + 8 + i * (2 * z - 1)
+                    send(SX, sx, sx, {"wide_0": lax.rem(at, 8), "narrow_1": c})
+
+    @pl.when(jnp.logical_not(is_root))
+    def _():
+        arrived(SX, sx)
+
+    scale = jnp.sum(jnp.where(lane == sub, jnp.broadcast_to(sx[...], (8, 128)), 0.0), axis=1, keepdims=True)
     cscs[...] = inv_s * scale[0:4]
     cscn[...] = inv_n * scale[4:8]
 
     drained(ROWS, rows_buf.at[pl.ds(1, 7)])
 
     def drain_owner():
-        drained(CZ, c_out.at[pl.ds(0, OWNERS - 1)])
-        drained(WZ, w_out.at[pl.ds(0, OWNERS - 1)])
+        if OWNERS > 1:
+            drained(CZ, c_out.at[pl.ds(0, OWNERS - 1)])
+            drained(WZ, w_out.at[pl.ds(0, OWNERS - 1)])
         drained(CY, cy.at[pl.ds(0, 7)])
-        drained(WY, wy.at[pl.ds(0, 7)])
         drained(AG, cz.at[pl.ds(0, 15)])
-        drained(SX, part.at[0, pl.ds(0, 126)])
+
+        @pl.when(is_root)
+        def _():
+            drained(TX, tx.at[pl.ds(0, len(ROOTS) - 1)])
+            drained(SX, part.at[0, pl.ds(0, 2 * len(SERVED) - 1)])
+
+        @pl.when(jnp.logical_not(is_root))
+        def _():
+            drained(TX, tx.at[pl.ds(0, len(ROOTS))])
 
     def drain_other():
         drained(CZ, c_out)
@@ -342,9 +363,9 @@
             V((8, 8, 128), f32),
             V((OWNERS, CR, 128), f32), V((OWNERS, WR, 128), f32),
             V((16, CR, 128), f32), V((8, CR2, 128), f32),
-            V((16, WR, 128), f32), V((8, WR2, 128), f32),
+            V((16, WR, 128), f32), V((1, WR2, 128), f32),
             V((2, CR, 128), f32), V((OWNERS, CR, 128), f32),
-            V((4 * OWNERS, 2, 128), f32),
+            V((32 * OWNERS, 1, 128), f32), V((1, 128), f32),
             pltpu.SemaphoreType.DMA((9,)),
             pltpu.SemaphoreType.DMA((7,)),
             pltpu.SemaphoreType.DMA((7,)),

time: 33.6 us -> 31.6 us (0.940)
  Pallas kernels: 32.9 us -> 30.8 us
    pallas_call x1, Pallas kernels: 31.3 us -> 29.3 us  [per_device(): pl.pallas_call(exchange_kernel, out_shape=[jax.ShapeDtypeStruct((4, 128,...]
where the time goes in v4:
time: 31.6 us; the launch traced here: 31.4 us
  Pallas kernels  30.8 us (97%)
  between operations  0.64 us (2%)
    pallas_call x1, Pallas kernels, per_device(): pl.pallas_call(exchange_kernel, out_shape=[jax.ShapeDtypeStruct((4, 128,...  29.3 us
    pallas_call x1, Pallas kernels, per_device(): pl.pallas_call(output_kernel, out_shape=[jax.ShapeDtypeStruct((4, 128, 10...  1.51 us

profile of v4, /device:TPU:1, one launch (start us, length us, event | category | flops | bytes accessed | tf_op | source)
XLA Modules:
  0.0 31.4 jit_solution(15160568813625971605)
XLA Ops:
  0.6 29.3 %exchange.1 = (f32[4,128,1024]{2,1,0:T(8,128)S(1)}, f32[4,128,128]{2,1,0:T(8,128)S(1)}, f32[8,128]{1,0:T(8,128)S(1)}, f32[4,1024]{1,0:T(4,128)S(1)}, f32[4,128]{...) custom-call(bf16[4,128,1024]{2,1,0:T(8,128)(2,1)} %gs.1, bf16[4,128,128]{2,1,0:T(8,128)(2,1)} %gn.1, ...), custom_call_target="tpu_custom_call" | custom-call | tf_op jit(solution)/shard_map/exchange/pallas_call | solution.py:349
  29.9 1.5 %output.1 = (f32[4,128,1024]{2,1,0:T(8,128)}, f32[4,128,128]{2,1,0:T(8,128)}, f32[4,128]{1,0:T(4,128)}, f32[4,1024]{1,0:T(4,128)}, f32[4,128]{1,0:T(4,128)}, /*index=5*/f32[4,128]{1,0:T(4,128)}) custom-call(f32[4,128,1024]{2,1,0:T(8,128)S(1)} %get-tuple-element.13.ts, f32[4,128,128]{2,1,0:T(8,128)S(1)} %get-tuple-element.14.tn, ...), custom_call_target="tpu_custom_call" | custom-call | tf_op jit(solution)/shard_map/output/pallas_call | solution.py:378

commit v5 on v4

--- a/solution.py
+++ b/solution.py
@@ -20,6 +20,7 @@
 
 ROWS, CZ, CY, WZ, AG, TX, SX = range(7)
 FAR_FIRST = (4, 3, 5, 2, 6, 1, 7)
+NARROW_FAR_FIRST = (5, 4, 3, 7, 2, 6, 1)
 
 OWNERS = 2
 OFFSET = 0
@@ -30,15 +31,17 @@
 WR = CR + 1
 CR2 = 2 * CR
 WR2 = CR2 + 1
-ROOT_ZS = (0, 1)
-ROOTS = [(t_z, t_y, t_x) for t_y in (0, 1, 2, 3, 7, 4, 6, 5) for t_z in ROOT_ZS for t_x in (0, 1, 3, 2)]
-SERVED = range(4) if len(ROOT_ZS) == 2 else (0, 1, 7, 2, 6, 3, 5, 4)
+ROOTS = [root for t_y in (0, 1, 2, 3, 7, 4, 6, 5) for root in
+         [(0, t_y, t_x, 1) for t_x in (0, 1, 3, 2)]
+         + [(0, t_y, t_x, 0) for t_x in (0, 1, 3, 2)]
+         + [(1, t_y, t_x, 1) for t_x in (0, 1, 3, 2)]]
+SERVED = [(1, 0)] + [(t_z, t_c) for t_z in (2, 7, 3, 6, 4, 5) for t_c in (1, 0)]
 
 
 def exchange_kernel(
     gs, gn, rs, rn, cs, cn,
     ts, tn, rowf, colfs, colfn, cscs, cscn,
-    vs, vn, vrs, vrn, vcs, vcn, part, rb,
+    vs, vn, vrs, vrn, vcs, vcn, qs, qn, part, rb,
     rows_buf, c_out, w_out, cz, cy, wz, w_all, own, ag, tx, sx,
     load_sem, send_sem, recv_sem,
 ):
@@ -47,7 +50,8 @@
     me = lax.rem(z + OFFSET, 8)
     on_plane = me < OWNERS
     is_owner = jnp.logical_and(on_plane, core == 1)
-    is_root = jnp.logical_and(z < len(ROOT_ZS), core == 1)
+    is_server = jnp.logical_and(z == 1, core == 1)
+    is_root = jnp.logical_or(z == 0, is_server)
 
     def on_y(d):
         return {"wide_1": lax.rem(y + d, 8)}
@@ -56,7 +60,7 @@
         return {"narrow_0": lax.rem(x + d // 2, 4), "narrow_1": lax.rem(core + d % 2, 2)}
 
     barrier = pltpu.get_barrier_semaphore()
-    for d in FAR_FIRST:
+    for d in NARROW_FAR_FIRST:
         pl.semaphore_signal(barrier, inc=1, device_id=on_narrow(d), device_id_type=MESH)
 
     loads = [pltpu.make_async_copy(gs.at[m], vs.at[m], load_sem.at[m]) for m in range(4)]
@@ -104,21 +108,18 @@
             def _():
                 send(kind, out.at[o], buf.at[z * 2 + core], {"wide_0": at, "narrow_1": 1})
 
-    def column_sums(m, ref, width):
+    def row_sums(m, ref, out, width):
         blocks = width // 128
-
-        def step(r, acc):
+        for r in range(8):
             rows = pl.ds(r * 16, 16)
-            v = ref[rows, :].astype(f32)
-            q = v * v
-            p = q[:, 0:128]
-            for b in range(1, blocks):
-                p = p + q[:, b * 128:(b + 1) * 128]
+            p = None
+            for b in range(blocks):
+                v = ref[rows, b * 128:(b + 1) * 128].astype(f32)
+                q = v * v
+                out[rows, b * 128:(b + 1) * 128] = q
+                p = q if p is None else p + q
             part[m, rows, :] = p
-            return acc + (q[0:8] + q[8:16])
-
-        acc = lax.fori_loop(0, 8, step, jnp.zeros((8, width), f32), unroll=True)
-        return jnp.sum(acc, axis=0, keepdims=True)
+        rows_buf[0, m:m + 1, :] = jnp.sum(part[m].T, axis=0, keepdims=True)
 
     def place_square(out, m, k, row):
         r = (k % BLOCKS) * 4 + m
@@ -130,26 +131,39 @@
                 if (o * NARROWS + i) % 4 == m:
                     out[o, SQ + i:SQ + i + 1, :] = row
 
-    old = decay_rate / (1.0 - decay_rate) * 8192 / 64
     for m in range(4):
         loads[m].wait()
-        if m == 0:
-            for c in loads[5:]:
-                c.wait()
-        total = column_sums(m, vs.at[m], 1024) + old * vcs[m:m + 1, :]
-        for k in range(8):
-            place_square(c_out, m, k, total[:, k * 128:(k + 1) * 128])
+        row_sums(m, vs.at[m], qs.at[m], 1024)
     loads[4].wait()
     for m in range(4):
-        place_narrow(c_out, m, column_sums(4 + m, vn.at[m], 128) + old * vcn[m:m + 1, :])
-    for m in range(8):
-        rows_buf[0, m:m + 1, :] = jnp.sum(part[m].T, axis=0, keepdims=True)
+        row_sums(4 + m, vn.at[m], qn.at[m], 128)
 
     others = jnp.where(on_plane, OWNERS - 1, OWNERS)
     pl.semaphore_wait(barrier, 7 + others + jnp.where(is_owner, 7, 0))
 
-    for d in FAR_FIRST:
+    for d in NARROW_FAR_FIRST:
         send(ROWS, rows_buf.at[0], rows_buf.at[d], on_narrow(d))
+
+    def column_sums(ref, width, weight=None):
+        acc = [None] * (width // 128)
+        for r in range(16):
+            rows = pl.ds(r * 8, 8)
+            w = None if weight is None else weight[rows, :] * weight[rows, :]
+            for b in range(width // 128):
+                q = ref[rows, b * 128:(b + 1) * 128]
+                q = q if w is None else q * w
+                acc[b] = q if acc[b] is None else acc[b] + q
+        return [jnp.sum(a, axis=0, keepdims=True) for a in acc]
+
+    for c in loads[5:]:
+        c.wait()
+    old = decay_rate / (1.0 - decay_rate) * 8192 / 64
+    for m in range(4):
+        total = column_sums(qs.at[m], 1024)
+        for k in range(8):
+            place_square(c_out, m, k, total[k] + old * vcs[m:m + 1, k * 128:(k + 1) * 128])
+    for m in range(4):
+        place_narrow(c_out, m, column_sums(qn.at[m], 128)[0] + old * vcn[m:m + 1, :])
     to_owners(CZ, c_out, cz)
 
     arrived(ROWS, rows_buf.at[pl.ds(1, 7)])
@@ -172,31 +186,23 @@
     for o in range(OWNERS):
         w_out[o, CR:CR + 1, :] = totals
 
-    def weighted_sums(m, ref, out, width):
-        blocks = width // 128
-
-        def step(r, acc):
+    for m in range(4):
+        total = column_sums(qs.at[m], 1024, rb.at[m])
+        for k in range(8):
+            place_square(w_out, m, k, total[k])
+    for m in range(4):
+        place_narrow(w_out, m, column_sums(qn.at[m], 128, rb.at[4 + m])[0])
+    to_owners(WZ, w_out, wz)
+    for m in range(8):
+        for r in range(8):
             rows = pl.ds(r * 16, 16)
             scale = rb[m, rows, :]
-            v = ref[rows, :].astype(f32)
-            new = []
-            for b in range(blocks):
-                t = v[:, b * 128:(b + 1) * 128] * scale
-                out[rows, b * 128:(b + 1) * 128] = t
-                q = t * t
-                new.append(acc[b] + (q[0:8] + q[8:16]))
-            return tuple(new)
-
-        acc = lax.fori_loop(0, 8, step, tuple(jnp.zeros((8, 128), f32) for _ in range(blocks)), unroll=True)
-        return [jnp.sum(a, axis=0, keepdims=True) for a in acc]
-
-    for m in range(4):
-        total = weighted_sums(m, vs.at[m], ts.at[m], 1024)
-        for k in range(8):
-            place_square(w_out, m, k, total[k])
-    for m in range(4):
-        place_narrow(w_out, m, weighted_sums(4 + m, vn.at[m], tn.at[m], 128)[0])
-    to_owners(WZ, w_out, wz)
+            if m < 4:
+                for b in range(8):
+                    columns = slice(b * 128, (b + 1) * 128)
+                    ts[m, rows, columns] = vs[m, rows, columns].astype(f32) * scale
+            else:
+                tn[m - 4, rows, :] = vn[m - 4, rows, :].astype(f32) * scale
 
     def over_z(kind, out, buf, into, slot):
         arrived(kind, buf.at[pl.ds(0, 15)])
@@ -241,10 +247,14 @@
         share = jnp.sum(jnp.where(lanec == target, share, 0.0), axis=0, keepdims=True)
         tx[slot] = share + weighted[CR2:WR2]
         mine = tx.at[slot]
-        for t_z, t_y, t_x in ROOTS:
-            @pl.when(jnp.logical_or(jnp.logical_or(z != t_z, y != t_y), x != t_x))
-            def _():
-                send(TX, mine, mine, {"wide_0": t_z, "wide_1": t_y, "narrow_0": t_x})
+        for t_z, t_y, t_x, t_c in ROOTS:
+            peer = {"wide_0": t_z, "wide_1": t_y, "narrow_0": t_x, "narrow_1": t_c}
+            if t_c == 0:
+                send(TX, mine, mine, peer)
+            else:
+                @pl.when(jnp.logical_or(jnp.logical_or(z != t_z, y != t_y), x != t_x))
+                def _():
+                    send(TX, mine, mine, peer)
 
     def owner_arrived():
         if OWNERS > 1:
@@ -263,7 +273,7 @@
 
     @pl.when(is_root)
     def _():
-        arrived(TX, tx.at[pl.ds(0, 32 * OWNERS - 1)])
+        if_owner(lambda: arrived(TX, tx.at[pl.ds(0, 32 * OWNERS - 1)]), lambda: arrived(TX, tx))
         sums = [tx[i] for i in range(4)]
         for i in range(4, 32 * OWNERS):
             sums[i % 4] = sums[i % 4] + tx[i]
@@ -272,11 +282,11 @@
         row_mean = pltpu.roll(pair, 128 - 8, 1) / (4 * OWNERS * 8192)
         spread = jnp.sqrt(row_mean * pair / entries)
         sx[...] = jnp.sqrt(row_mean) / jnp.maximum(1.0, spread / clip_limit)
-        for i in SERVED:
-            for c in (1, 0):
-                if (i, c) != (0, 1):
-                    at = z + i if len(ROOT_ZS) == 1 else z + 8 + i * (2 * z - 1)
-                    send(SX, sx, sx, {"wide_0": lax.rem(at, 8), "narrow_1": c})
+
+        @pl.when(is_server)
+        def _():
+            for t_z, t_c in SERVED:
+                send(SX, sx, sx, {"wide_0": t_z, "narrow_1": t_c})
 
     @pl.when(jnp.logical_not(is_root))
     def _():
@@ -295,14 +305,11 @@
         drained(CY, cy.at[pl.ds(0, 7)])
         drained(AG, cz.at[pl.ds(0, 15)])
 
-        @pl.when(is_root)
+        drained(TX, part.at[0, pl.ds(0, len(ROOTS) - 1)])
+
+        @pl.when(is_server)
         def _():
-            drained(TX, tx.at[pl.ds(0, len(ROOTS) - 1)])
-            drained(SX, part.at[0, pl.ds(0, 2 * len(SERVED) - 1)])
-
-        @pl.when(jnp.logical_not(is_root))
-        def _():
-            drained(TX, tx.at[pl.ds(0, len(ROOTS))])
+            drained(SX, part.at[0, pl.ds(0, len(SERVED))])
 
     def drain_other():
         drained(CZ, c_out)
@@ -359,6 +366,7 @@
         scratch_shapes=[
             V((4, 128, 1024), jnp.bfloat16), V((4, 128, 128), jnp.bfloat16),
             V((4, 128), f32), V((4, 128), f32), V((4, 1024), f32), V((4, 128), f32),
+            V((4, 128, 1024), f32), V((4, 128, 128), f32),
             V((8, 128, 128), f32), V((8, 128, 128), f32),
             V((8, 8, 128), f32),
             V((OWNERS, CR, 128), f32), V((OWNERS, WR, 128), f32),

time: 31.6 us -> 30.7 us (0.972)
  Pallas kernels: 30.8 us -> 29.9 us
    pallas_call x1, Pallas kernels: 29.3 us -> 28.4 us  [per_device(): pl.pallas_call(exchange_kernel, out_shape=[jax.ShapeDtypeStruct((4, 128,...]
where the time goes in v5:
time: 30.7 us; the launch traced here: 30.6 us
  Pallas kernels  29.9 us (97%)
  between operations  0.64 us (2%)
    pallas_call x1, Pallas kernels, per_device(): pl.pallas_call(exchange_kernel, out_shape=[jax.ShapeDtypeStruct((4, 128,...  28.4 us
    pallas_call x1, Pallas kernels, per_device(): pl.pallas_call(output_kernel, out_shape=[jax.ShapeDtypeStruct((4, 128, 10...  1.51 us

profile of v5, /device:TPU:1, one launch (start us, length us, event | category | flops | bytes accessed | tf_op | source)
XLA Modules:
  0.0 30.6 jit_solution(16189719668651036885)
XLA Ops:
  0.6 28.4 %exchange.1 = (f32[4,128,1024]{2,1,0:T(8,128)S(1)}, f32[4,128,128]{2,1,0:T(8,128)S(1)}, f32[8,128]{1,0:T(8,128)S(1)}, f32[4,1024]{1,0:T(4,128)S(1)}, f32[4,128]{...) custom-call(bf16[4,128,1024]{2,1,0:T(8,128)(2,1)} %gs.1, bf16[4,128,128]{2,1,0:T(8,128)(2,1)} %gn.1, ...), custom_call_target="tpu_custom_call" | custom-call | tf_op jit(solution)/shard_map/exchange/pallas_call | solution.py:356
  29.1 1.5 %output.1 = (f32[4,128,1024]{2,1,0:T(8,128)}, f32[4,128,128]{2,1,0:T(8,128)}, f32[4,128]{1,0:T(4,128)}, f32[4,1024]{1,0:T(4,128)}, f32[4,128]{1,0:T(4,128)}, /*index=5*/f32[4,128]{1,0:T(4,128)}) custom-call(f32[4,128,1024]{2,1,0:T(8,128)S(1)} %get-tuple-element.13.ts, f32[4,128,128]{2,1,0:T(8,128)S(1)} %get-tuple-element.14.tn, ...), custom_call_target="tpu_custom_call" | custom-call | tf_op jit(solution)/shard_map/output/pallas_call | solution.py:386
